TPU v7x, 32 devices: a whole 2x2x4 slice. The times are simulated.
32 devices in a mesh: member: 2 (over x), band: 16 (over z, y, core).
Axes of the slice: x: 2, y: 2, z: 4, core: 2. Of those that a mesh axis runs over, the one named last changes fastest.
Arguments:
- grid_in: bfloat16 [32, 274, 5248], P(('member', 'band')), parts along dimension 0, may hold values from -6 to 6
- legendre: bfloat16 [16, 2, 640, 8], P('band'), may hold values from -2 to 2
- gauss_weight: float32 [8], replicated, may hold values from 0.2 to 2
- vertical_modes: float32 [137, 137], replicated
- coupling: float32 [137, 137], replicated, may hold values from -0.5 to 0.5
- mode_rates: float32 [137], replicated, may hold values from 0.1 to 10
- loop_length: int32 [16], replicated, may hold values from 20 to 5136, as said below
- lat_order: int32 [16], replicated, may hold values from 0 to 15, each once
- wave_number: int32 [16], replicated, may hold values from 0 to 1279, as said below
Outputs:
- grid_out: bfloat16 [32, 274, 5248], P(('member', 'band')), parts along dimension 0
There are 2 independent parts, one for each index of `member`. A program takes and returns all parts, laid end to end along the dimension named above; an argument that names none is the same for every part. Nothing has to cross between parts.
Inputs may be any that keep to these rules, and one draw needn't show every extreme that they name: loop_length[t] = 20 + 4 k with k not falling from the poles toward the equator, equal for latitudes t and 15 - t; the equatorial loops have 5248 - 112 points. Row i of grid_in and grid_out holds latitude lat_order[i]. `wave_number`: distinct values.
All inputs are finite; a program needn't handle non-finite values.
Results may differ from a plain program's by a relative error of at most 0.013.
Values may be sent and summed in bfloat16 or wider, within the bound.
A program may use at most 64 MiB of HBM per device.

v0:
```python
import math
import jax
import jax.numpy as jnp
from jax import lax
from jax.sharding import PartitionSpec as P

TRUNC = 1279
implicit_step = 0.5
highest = lax.Precision.HIGHEST


def loop_tables(length, wave_list, block_count):
    offsets = jnp.arange(128, dtype=jnp.int32)
    inner_turn = offsets[:, None] * wave_list[None, :] % length
    angles = inner_turn.astype(jnp.float32) * (2.0 * math.pi) / length.astype(jnp.float32)
    inner_table = jnp.concatenate([jnp.cos(angles), jnp.sin(angles)], axis=1).astype(jnp.bfloat16)
    block_index = jnp.arange(block_count, dtype=jnp.int32)
    outer_turn = block_index[:, None] * 128 * wave_list[None, :] % length
    phases = outer_turn.astype(jnp.float32) * (2.0 * math.pi) / length.astype(jnp.float32)
    return (inner_table, jnp.cos(phases), jnp.sin(phases))


def forward_loop(one_loop, length, wave_list):
    field_count, loop_width = one_loop.shape
    block_count = loop_width // 128
    wave_count = wave_list.shape[0]
    inner_table, cos_turn, sin_turn = loop_tables(length, wave_list, block_count)
    inside = jnp.arange(loop_width, dtype=jnp.int32) < length
    masked = jnp.where(inside[None, :], one_loop, jnp.zeros((), one_loop.dtype))
    products = jnp.dot(
        masked.reshape(field_count * block_count, 128),
        inner_table,
        preferred_element_type=jnp.float32,
    )
    products = products.reshape(field_count, block_count, 2, wave_count)
    real_part = jnp.sum(cos_turn * products[:, :, 0] - sin_turn * products[:, :, 1], axis=1)
    imag_part = -jnp.sum(sin_turn * products[:, :, 0] + cos_turn * products[:, :, 1], axis=1)
    inverse_len = 1.0 / length.astype(jnp.float32)
    together = jnp.concatenate([real_part, imag_part], axis=0) * inverse_len
    resolved = 2 * wave_list < length
    together = jnp.where(resolved[None, :], together, 0.0)
    return together.T.astype(jnp.bfloat16)


def inverse_loop(fourier, length, wave_list, loop_width):
    block_count = loop_width // 128
    wave_count = wave_list.shape[0]
    field_count = fourier.shape[1] // 2
    inner_table, cos_turn, sin_turn = loop_tables(length, wave_list, block_count)
    doubling = jnp.where(wave_list == 0, 1.0, 2.0).astype(jnp.float32)
    real_part = fourier[:, :field_count].astype(jnp.float32).T * doubling
    imag_part = fourier[:, field_count:].astype(jnp.float32).T * doubling
    cosine_part = real_part[:, None, :] * cos_turn[None] - imag_part[:, None, :] * sin_turn[None]
    sine_part = -(real_part[:, None, :] * sin_turn[None] + imag_part[:, None, :] * cos_turn[None])
    combined = jnp.concatenate([cosine_part, sine_part], axis=2).astype(jnp.bfloat16)
    points = lax.dot_general(
        combined.reshape(field_count * block_count, 2 * wave_count),
        inner_table,
        (((1,), (1,)), ((), ())),
        preferred_element_type=jnp.float32,
    )
    points = points.reshape(field_count, loop_width)
    inside = jnp.arange(loop_width, dtype=jnp.int32) < length
    return jnp.where(inside[None, :], points, 0.0).astype(jnp.bfloat16)


def semi_implicit(spectral, wave_values, vertical_modes, coupling, mode_rates):
    half_rows = spectral.shape[-2]
    level_count = vertical_modes.shape[0]
    parity = jnp.arange(2, dtype=jnp.int32)
    row_index = jnp.arange(half_rows, dtype=jnp.int32)
    degree = wave_values[..., None, None] + parity[:, None] + 2 * row_index[None, :]
    kept_rows = degree <= TRUNC
    spectral = jnp.where(kept_rows[..., None], spectral, 0.0)
    damping = (degree * (degree + 1)).astype(jnp.float32) / float(TRUNC * (TRUNC + 1))
    reshaped = spectral.reshape(spectral.shape[:-1] + (2, 2, level_count))
    divergence = reshaped[..., 0, :]
    pressure = reshaped[..., 1, :]
    factor_e = damping[..., None, None]
    right_side = divergence - implicit_step * factor_e * jnp.einsum(
        "...l,kl->...k", pressure, coupling, precision=highest
    )
    in_modes = jnp.einsum("...l,lk->...k", right_side, vertical_modes, precision=highest)
    in_modes = in_modes / (1.0 + implicit_step * factor_e * mode_rates)
    new_div = jnp.einsum("...k,lk->...l", in_modes, vertical_modes, precision=highest)
    new_press = pressure - implicit_step * jnp.einsum(
        "...l,kl->...k", new_div, coupling, precision=highest
    )
    updated = jnp.stack([new_div, new_press], axis=-2)
    return updated.reshape(spectral.shape).astype(jnp.bfloat16)


def per_device(
    grid_in,
    legendre,
    gauss_weight,
    vertical_modes,
    coupling,
    mode_rates,
    loop_length,
    lat_order,
    wave_number,
):
    groups = lax.axis_size("band")
    band_index = lax.axis_index("band")
    loop_count, field_count, loop_width = grid_in.shape
    slot_count = legendre.shape[0]
    lat_count = lat_order.shape[0]
    half_count = lat_count // 2
    column_count = 2 * field_count
    wave_total = wave_number.shape[0]
    own_rows = lax.dynamic_slice_in_dim(lat_order, band_index * loop_count, loop_count)
    own_lengths = jnp.take(loop_length, own_rows)
    column_waves = wave_number.reshape(groups, slot_count).T.reshape(wave_total)
    own_waves = lax.dynamic_slice_in_dim(wave_number, band_index * slot_count, slot_count)

    def forward_piece(scan_carry, scan_item):
        one_loop, length = scan_item
        loop_piece = forward_loop(one_loop, length, column_waves).reshape(
            slot_count, groups, column_count
        )
        return (
            scan_carry,
            lax.all_to_all(loop_piece, "band", split_axis=1, concat_axis=1, tiled=True),
        )

    unused, pieces = lax.scan(forward_piece, 0, (grid_in, own_lengths))
    arrived = jnp.transpose(pieces, (1, 2, 0, 3))
    arrived = arrived.reshape(slot_count, lat_count, column_count)
    row_of_lat = jnp.argsort(lat_order)
    northern = jnp.take(arrived, row_of_lat[:half_count], axis=1).astype(jnp.float32)
    southern = jnp.take(arrived, row_of_lat[::-1][:half_count], axis=1).astype(jnp.float32)
    weight = gauss_weight[None, :, None]
    even_part = (weight * (northern + southern)).astype(jnp.bfloat16)
    odd_part = (weight * (northern - southern)).astype(jnp.bfloat16)
    stacked = jnp.stack([even_part, odd_part], axis=1)
    spectral = jnp.einsum("kprj,kpjc->kprc", legendre, stacked, preferred_element_type=jnp.float32)
    updated = semi_implicit(spectral, own_waves, vertical_modes, coupling, mode_rates)
    summed = jnp.einsum("kprj,kprc->kpjc", legendre, updated, preferred_element_type=jnp.float32)
    northern_back = summed[:, 0] + summed[:, 1]
    southern_back = summed[:, 0] - summed[:, 1]
    by_lat = jnp.concatenate([northern_back, southern_back[:, ::-1]], axis=1)
    resolved = 2 * own_waves[:, None] < loop_length[None, :]
    by_lat = jnp.where(resolved[:, :, None], by_lat, 0.0).astype(jnp.bfloat16)
    returning = jnp.take(by_lat, lat_order, axis=1).reshape(
        slot_count, groups, loop_count, column_count
    )
    outgoing_loops = jnp.transpose(returning, (2, 0, 1, 3))

    def inverse_piece(scan_carry, scan_item):
        loop_data, length = scan_item
        loop_back = lax.all_to_all(loop_data, "band", split_axis=1, concat_axis=1, tiled=True)
        return (
            scan_carry,
            inverse_loop(
                loop_back.reshape(wave_total, column_count), length, column_waves, loop_width
            ),
        )

    unused, grid_out = lax.scan(inverse_piece, 0, (outgoing_loops, own_lengths))
    return grid_out


def solution(mesh):
    placed = (
        P(("member", "band"), None, None),
        P("band", None, None, None),
        P(),
        P(),
        P(),
        P(),
        P(),
        P(),
        P(),
    )
    return jax.shard_map(
        per_device,
        mesh=mesh,
        in_specs=placed,
        out_specs=P(("member", "band"), None, None),
        check_vma=False,
    )
```

profile of v0, /device:TPU:0, one launch (start us, length us, event | category | flops | bytes accessed | tf_op | source)
XLA Modules:
  0.0 72.8 jit_solution(2726533253867949105)
XLA Ops:
  0.0 1.3 %dynamic_slice.17 = s32[1]{0:T(128)} dynamic-slice(s32[16]{0:T(128)} %param.18, s32[]{:T(128)S(6)} %select_n.129), dynamic_slice_sizes={1} | dynamic-slice | bytes 12 | tf_op jit(solution)/shard_map/dynamic_slice | solution.py:112
  3.2 1.3 %dynamic-slice.3 = s32[1]{0:T(128)} dynamic-slice(s32[16]{0:T(128)} %param.17, s32[]{:T(128)} %bitcast), dynamic_slice_sizes={1} | dynamic-slice | bytes 12 | tf_op jit(solution)/shard_map/jit(_take)/gather | solution.py:113
  5.8 3.7 %broadcast_select_fusion = bf16[1,274,5248]{2,1,0:T(8,128)(2,1)} fusion(bf16[1,274,5248]{2,1,0:T(8,128)(2,1)} %param.11, pred[5248]{0:T(1024)(128)(4,1)S(1)} %iota_compare_fusion), kind=kLoop, calls=%fused_computation.6 | loop fusion | flops 1437952 | bytes 5757056 | tf_op jit(solution)/shard_map/while/body/eval_jaxpr/jit(_where)/select_n | solution.py:29
  9.4 4.2 %select_n.136 = bf16[274,41,128]{2,1,0:T(8,128)(2,1)S(1)} reshape(bf16[1,274,5248]{2,1,0:T(8,128)(2,1)} %broadcast_select_fusion) | data formatting | bytes 5751808 | tf_op jit(solution)/shard_map/while/body/eval_jaxpr/jit(_where)/select_n | solution.py:29
  14.4 1.1 %fusion.46 = (f32[41,16]{1,0:T(8,128)S(1)}, f32[41,16]{1,0:T(8,128)S(1)}) fusion(f32[]{:T(128)S(6)} %convert_element_type.103, pred[]{:T(512)S(6)} %lt.94, s32[]{:T(128)S(6)} %select_n.133, s32[16]{0:T(128)} %param.19, s32[41]{0:T(128)} %iota_multiply_fusion.1), kind=kLoop, calls=%fused_computation.77 | loop fusion | flops 7216 | bytes 5485 | tf_op jit(solution)/shard_map/while/body/eval_jaxpr/cos | solution.py:20
  15.5 1.6 %fusion = f32[274,41,2,16]{0,3,2,1:T(8,128)S(1)} fusion(bf16[2,16,128,1]{2,1,0,3:T(8,128)(2,1)S(1)} %bitcast.133, bf16[274,41,128,1]{2,1,0,3:T(8,128)(2,1)S(1)} %bitcast.123), kind=kOutput, calls=%fused_computation.4 | convolution fusion | flops 92028928 | bytes 4322048 | tf_op jit(solution)/shard_map/while/body/eval_jaxpr/dot_general | solution.py:30
  19.1 0.7 reshape.543
  19.8 7.4 %all-to-all-start = ((bf16[16,2,274]{2,1,0:T(2,128)(2,1)}), bf16[16,2,274]{2,1,0:T(2,128)(2,1)S(1)}, u32[]{:S(2)}, u32[]{:S(2)}) async-start(bf16[16,2,274]{2,1,0:T(2,128)(2,1)} %reshape.543), calls=%async_computation | async-start | bytes 49152 | tf_op jit(solution)/shard_map/while/body/eval_jaxpr/all_to_all | solution.py:124
  27.2 1.3 %sort.17 = (s32[16]{0:T(128)}, s32[16]{0:T(128)S(1)}) sort(s32[16]{0:T(128)S(1)} %copy-done.10, s32[16]{0:T(128)S(1)} %iota.42), dimensions={0}, to_apply=%region_2.3 | sort | flops 64 | bytes 256 | tf_op jit(solution)/shard_map/jit(argsort)/sort | solution.py:130
  31.1 2.6 %all-to-all-done = bf16[16,2,274]{2,1,0:T(2,128)(2,1)S(1)} async-done(((bf16[16,2,274]{2,1,0:T(2,128)(2,1)}), bf16[16,2,274]{2,1,0:T(2,128)(2,1)S(1)}, u32[]{:S(2)}, u32[]{:S(2)}) %all-to-all-start) | async-done | bytes 17568 | tf_op jit(solution)/shard_map/while/body/eval_jaxpr/all_to_all | solution.py:124
  35.8 1.4 %copy.35 = f32[2,640,548]{1,0,2:T(2,128)S(1)} copy(f32[2,640,548]{1,2,0:T(8,128)S(1)} %select_bitcast_fusion) | data formatting | bytes 5611520 | tf_op jit(solution)/shard_map/jit(_where)/select_n | solution.py:74
  37.2 1.0 %fusion.60 = (f32[1,2,640,2,1,137]{2,1,5,4,3,0:T(2,128)S(1)}, f32[1,2,640,2,1,137]{2,1,5,4,3,0:T(2,128)S(1)}) fusion(f32[1,2,640,2,2,137]{2,1,5,4,3,0:T(2,128)S(1)} %bitcast.124), kind=kLoop, calls=%fused_computation.115 | loop fusion | bytes 5611520 | tf_op jit(solution)/shard_map/slice | solution.py:78
  38.2 1.4 %fusion.8 = f32[2,640,2,137]{1,3,2,0:T(8,128)S(1)} fusion(f32[1,2,640,2,1,137]{2,1,5,4,3,0:T(2,128)S(1)} %get-tuple-element.53, f32[137,137]{1,0:T(8,128)S(1)} %copy-done.1), kind=kOutput, calls=%fused_computation.17 | convolution fusion | flops 576583680 | bytes 2880836 | tf_op jit(solution)/shard_map/...l,kl->...k/dot_general | solution.py:80
  39.7 1.6 %fusion.3 = f32[2,640,2,137]{1,3,2,0:T(8,128)S(1)} fusion(f32[1,2,640,2,1,137]{2,1,5,4,3,0:T(2,128)S(1)} %get-tuple-element.54, f32[2,640,2,137]{1,3,2,0:T(8,128)S(1)} %fusion.8, f32[2,640]{1,0:T(2,128)S(1)} %fusion.57, f32[137,137]{1,0:T(8,128)S(1)} %copy-done), kind=kOutput, calls=%fused_computation.12 | convolution fusion | flops 577285120 | bytes 4288836 | tf_op jit(solution)/shard_map/...l,lk->...k/dot_general | solution.py:83
  41.3 1.6 %fusion.5 = f32[2,640,2,137]{1,3,2,0:T(8,128)S(1)} fusion(f32[2,640,2,137]{1,3,2,0:T(8,128)S(1)} %fusion.3, f32[2,640,137]{1,2,0:T(8,128)S(1)} %multiply_add_fusion, f32[137,137]{1,0:T(8,128)S(1)} %copy-done), kind=kOutput, calls=%fused_computation.14 | convolution fusion | flops 576934400 | bytes 3582276 | tf_op jit(solution)/shard_map/...k,lk->...l/dot_general | solution.py:85
  43.0 1.5 %fusion.11 = bf16[1,2,640,2,1,137]{2,5,3,1,4,0:T(8,128)(2,1)S(1)} fusion(f32[2,640,2,137]{1,3,2,0:T(8,128)S(1)} %fusion.5, f32[1,2,640,2,1,137]{2,1,5,4,3,0:T(2,128)S(1)} %get-tuple-element.53, f32[137,137]{1,0:T(8,128)S(1)} %copy-done.1), kind=kOutput, calls=%fused_computation.20 | convolution fusion | flops 577635840 | bytes 3582276 | tf_op jit(solution)/shard_map/...l,kl->...k/dot_general | solution.py:86
  44.7 1.1 %copy.39 = bf16[1,2,640,2,2,137]{2,1,5,4,3,0:T(2,128)(2,1)S(1)} copy(bf16[1,2,640,2,2,137]{2,5,3,1,4,0:T(8,128)(2,1)S(1)} %pad_maximum_fusion) | data formatting | bytes 2805760 | tf_op jit(solution)/shard_map/stack | solution.py:89
  48.6 3.7 %all-to-all-start.1 = ((bf16[16,2,274]{2,1,0:T(2,128)(2,1)}), bf16[16,2,274]{2,1,0:T(2,128)(2,1)S(1)}, u32[]{:S(2)}, u32[]{:S(2)}) async-start(bf16[16,2,274]{2,1,0:T(2,128)(2,1)} %reshape.545), calls=%async_computation.1 | async-start | bytes 49152 | tf_op jit(solution)/shard_map/while/body/eval_jaxpr/all_to_all | solution.py:152
  52.3 6.3 %all-to-all-done.1 = bf16[16,2,274]{2,1,0:T(2,128)(2,1)S(1)} async-done(((bf16[16,2,274]{2,1,0:T(2,128)(2,1)}), bf16[16,2,274]{2,1,0:T(2,128)(2,1)S(1)}, u32[]{:S(2)}, u32[]{:S(2)}) %all-to-all-start.1) | async-done | bytes 17568 | tf_op jit(solution)/shard_map/while/body/eval_jaxpr/all_to_all | solution.py:152
  59.2 0.9 %copy.43 = bf16[274,41,16]{1,0,2:T(8,128)(2,1)S(1)} copy(bf16[274,41,16]{0,2,1:T(8,128)(2,1)S(1)} %get-tuple-element.56) | data formatting | bytes 718976 | tf_op jit(solution)/shard_map/convert.2
  60.7 0.9 %copy.42 = bf16[274,41,16]{1,0,2:T(8,128)(2,1)S(1)} copy(bf16[274,41,16]{0,2,1:T(8,128)(2,1)S(1)} %get-tuple-element.55) | data formatting | bytes 718976 | tf_op jit(solution)/shard_map/convert.3
  62.3 3.3 %fusion.17 = bf16[11234,128]{1,0:T(8,128)(2,1)} fusion(bf16[11234,16]{0,1:T(8,128)(2,1)S(1)} %neg.14, bf16[11234,16]{0,1:T(8,128)(2,1)S(1)} %sub.44, bf16[128,16]{0,1:T(8,128)(2,1)S(1)} %get-tuple-element.66, bf16[128,16]{0,1:T(8,128)(2,1)S(1)} %get-tuple-element.65), kind=kOutput, calls=%fused_computation.32 | convolution fusion | flops 93483264 | bytes 3603072 | tf_op jit(solution)/shard_map/while/body/eval_jaxpr/dot_general | solution.py:56
  65.6 5.2 %reshape.469 = bf16[1,274,5248]{2,1,0:T(8,128)(2,1)S(1)} reshape(bf16[11234,128]{1,0:T(8,128)(2,1)} %fusion.17) | data formatting | bytes 5751808 | tf_op jit(solution)/shard_map/while/body/eval_jaxpr/reshape | solution.py:62
  70.7 2.1 %select_convert_fusion = bf16[1,274,5248]{2,1,0:T(8,128)(2,1)} fusion(bf16[1,274,5248]{2,1,0:T(8,128)(2,1)S(1)} %reshape.469, pred[5248]{0:T(1024)(128)(4,1)S(1)} %iota_compare_fusion), kind=kLoop, calls=%fused_computation.3 | loop fusion | flops 1437952 | bytes 5757056 | tf_op jit(solution)/shard_map/while/body/eval_jaxpr/convert_element_type | solution.py:64
  (76 shorter events, 11.8 us)
Async XLA Ops:
  0.0 39.7 %copy-start = (f32[137,137]{1,0:T(8,128)S(1)}, f32[137,137]{1,0:T(8,128)}, u32[]{:S(2)}) copy-start(f32[137,137]{1,0:T(8,128)} %param.14) | copy-start | bytes 225232
  9.4 4.2 %copy-start.5 = (s32[16]{0:T(128)S(1)}, s32[16]{0:T(128)}, u32[]{:S(2)}) copy-start(s32[16]{0:T(128)} %param.19) | copy-start | bytes 196
  15.5 1.7 %copy-start.2 = (f32[41,16]{1,0:T(8,128)}, f32[41,16]{1,0:T(8,128)S(1)}, u32[]{:S(2)}) copy-start(f32[41,16]{1,0:T(8,128)S(1)} %get-tuple-element.64) | copy-start | bytes 7876
  17.1 0.7 copy-start.9
  17.1 10.1 %copy-start.10 = (s32[16]{0:T(128)S(1)}, s32[16]{0:T(128)}, u32[]{:S(2)}) copy-start(s32[16]{0:T(128)} %param.18) | copy-start | bytes 196
  17.1 11.6 %copy-start.6 = (s32[16]{0:T(128)S(1)}, s32[16]{0:T(128)}, u32[]{:S(2)}) copy-start(s32[16]{0:T(128)} %param.19) | copy-start | bytes 196
  17.1 13.8 %copy-start.11 = (s32[16]{0:T(128)S(1)}, s32[16]{0:T(128)}, u32[]{:S(2)}) copy-start(s32[16]{0:T(128)} %param.17) | copy-start | bytes 196
  17.1 13.8 %copy-start.7 = (f32[137]{0:T(256)S(1)}, f32[137]{0:T(256)}, u32[]{:S(2)}) copy-start(f32[137]{0:T(256)} %param.16) | copy-start | bytes 1648
  17.2 17.9 %copy-start.8 = (f32[8]{0:T(128)S(1)}, f32[8]{0:T(128)}, u32[]{:S(2)}) copy-start(f32[8]{0:T(128)} %param.13) | copy-start | bytes 100
  17.2 17.9 %copy-start.4 = (bf16[1,2,640,8]{2,3,1,0:T(8,128)(2,1)S(1)}, bf16[1,2,640,8]{2,3,1,0:T(8,128)(2,1)}, u32[]{:S(2)}) copy-start(bf16[1,2,640,8]{2,3,1,0:T(8,128)(2,1)} %param.12) | copy-start | bytes 61444
  19.8 14.0 %all-to-all-start = ((bf16[16,2,274]{2,1,0:T(2,128)(2,1)}), bf16[16,2,274]{2,1,0:T(2,128)(2,1)S(1)}, u32[]{:S(2)}, u32[]{:S(2)}) async-start(bf16[16,2,274]{2,1,0:T(2,128)(2,1)} %reshape.543), calls=%async_computation | async-start | bytes 49152 | tf_op jit(solution)/shard_map/while/body/eval_jaxpr/all_to_all | solution.py:124
  37.2 1.0 %copy-start.1 = (f32[137,137]{1,0:T(8,128)S(1)}, f32[137,137]{1,0:T(8,128)}, u32[]{:S(2)}) copy-start(f32[137,137]{1,0:T(8,128)} %param.15) | copy-start | bytes 225232
  45.8 13.0 %copy-start.3 = (f32[41,16]{1,0:T(8,128)S(1)}, f32[41,16]{1,0:T(8,128)}, u32[]{:S(2)}) copy-start(f32[41,16]{1,0:T(8,128)} %copy-done.2) | copy-start | bytes 7876
  48.6 10.0 %all-to-all-start.1 = ((bf16[16,2,274]{2,1,0:T(2,128)(2,1)}), bf16[16,2,274]{2,1,0:T(2,128)(2,1)S(1)}, u32[]{:S(2)}, u32[]{:S(2)}) async-start(bf16[16,2,274]{2,1,0:T(2,128)(2,1)} %reshape.545), calls=%async_computation.1 | async-start | bytes 49152 | tf_op jit(solution)/shard_map/while/body/eval_jaxpr/all_to_all | solution.py:152
where the time goes:
time: 73.4 us; the launch traced here: 72.8 us
  local copies, waits for them, and re-layouts  23.6 us (32%)
  other arithmetic  13.2 us (18%)
  matrix products  12.1 us (16%)
  starting transfers between devices  11.1 us (15%)
  waiting for transfers between devices  8.92 us (12%)
  between operations  3.86 us (5%)
    all_to_all x1, starting transfers between devices, forward_piece(): lax.all_to_all(loop_piece, 'band', split_axis=1, concat_axis=1, tiled=True)  7.42 us
    all_to_all x1, waiting for transfers between devices, inverse_piece(): lax.all_to_all(loop_data, 'band', split_axis=1, concat_axis=1, tiled=True)  6.3 us
    reshape x1, local copies, waits for them, and re-layouts, inverse_loop(): points = points.reshape(field_count, loop_width)  5.17 us
    select_n x1, local copies, waits for them, and re-layouts, forward_loop(): masked = jnp.where(inside[None, :], one_loop, jnp.zeros((), one_loop.dtype))  4.15 us
    all_to_all x1, starting transfers between devices, inverse_piece(): lax.all_to_all(loop_data, 'band', split_axis=1, concat_axis=1, tiled=True)  3.72 us
    select_n x1, other arithmetic, forward_loop(): masked = jnp.where(inside[None, :], one_loop, jnp.zeros((), one_loop.dtype))  3.66 us
    dot_general x1, matrix products, inverse_loop(): lax.dot_general(combined.reshape(field_count * block_count, 2 * wave_coun...  3.28 us
    all_to_all x1, waiting for transfers between devices, forward_piece(): lax.all_to_all(loop_piece, 'band', split_axis=1, concat_axis=1, tiled=True)  2.62 us
  transfers between devices with their start and end apart: 2, of which 2 were waited for; matrix products, arithmetic and copies ran while one was open for 4% of the time, Pallas kernels for 0%

commit v1 on v0

--- a/solution.py
+++ b/solution.py
@@ -7,6 +7,18 @@
 TRUNC = 1279
 implicit_step = 0.5
 highest = lax.Precision.HIGHEST
+
+
+def in_blocks(shard, dim, length):
+    shape = shard.shape
+    tiles = shard.reshape(*shape[:dim], length, shape[dim] // length, *shape[dim + 1 :])
+    return jnp.moveaxis(tiles, dim, 0)
+
+
+def joined_along(tiles, dim):
+    tiles = jnp.moveaxis(tiles, 0, dim)
+    shape = tiles.shape
+    return tiles.reshape(*shape[:dim], shape[dim] * shape[dim + 1], *shape[dim + 2 :])
 
 
 def loop_tables(length, wave_list, block_count):
@@ -149,7 +161,17 @@
 
     def inverse_piece(scan_carry, scan_item):
         loop_data, length = scan_item
-        loop_back = lax.all_to_all(loop_data, "band", split_axis=1, concat_axis=1, tiled=True)
+        size, index = (lax.axis_size("band"), lax.axis_index("band"))
+        pieces_2 = in_blocks(loop_data, 1, size)
+        result = pieces_2
+        for step in range(1, size):
+            target, source = ((index + step) % size, (index - step) % size)
+            sent = lax.dynamic_index_in_dim(pieces_2, target, 0)
+            partner_block = lax.ppermute(
+                sent, "band", [(i, (i + step) % size) for i in range(size)]
+            )
+            result = lax.dynamic_update_slice_in_dim(result, partner_block, source, axis=0)
+        loop_back = joined_along(result, 1)
         return (
             scan_carry,
             inverse_loop(

time: 73.4 us -> 85.1 us (1.16)
  starting transfers between devices: 11.1 us -> 26.4 us
  waiting for transfers between devices: 8.92 us -> 5.16 us
    ppermute x0 -> x15, starting transfers between devices: none -> 18.9 us  [inverse_piece(): lax.ppermute(sent, 'band', [(i, (i + step) % size) for i in range(size)])]
    all_to_all x1 -> x0, waiting for transfers between devices: 6.3 us -> none  [inverse_piece(): lax.all_to_all(loop_data, 'band', split_axis=1, concat_axis=1, tiled=True)]
    all_to_all x1 -> x0, starting transfers between devices: 3.72 us -> none  [inverse_piece(): lax.all_to_all(loop_data, 'band', split_axis=1, concat_axis=1, tiled=True)]
    ppermute x0 -> x15, waiting for transfers between devices: none -> 2.89 us  [inverse_piece(): lax.ppermute(sent, 'band', [(i, (i + step) % size) for i in range(size)])]
    unnamed x31 -> x28, local copies, waits for them, and re-layouts: 2.35 us -> 1.55 us
  transfers between devices with their start and end apart: 2 -> 16, of which waited for: 2 -> 3; matrix products, arithmetic and copies ran while one was open for 4% -> 4% of each run, Pallas kernels for 0% -> 0%
where the time goes in v1:
time: 85.1 us; the launch traced here: 84.2 us
  starting transfers between devices  26.4 us (31%)
  local copies, waits for them, and re-layouts  23.5 us (28%)
  other arithmetic  12.6 us (15%)
  matrix products  12.1 us (14%)
  waiting for transfers between devices  5.16 us (6%)
  between operations  4.45 us (5%)
    ppermute x15, starting transfers between devices, inverse_piece(): lax.ppermute(sent, 'band', [(i, (i + step) % size) for i in range(size)])  18.9 us
    all_to_all x1, starting transfers between devices, forward_piece(): lax.all_to_all(loop_piece, 'band', split_axis=1, concat_axis=1, tiled=True)  7.42 us
    reshape x1, local copies, waits for them, and re-layouts, inverse_loop(): points = points.reshape(field_count, loop_width)  5.17 us
    select_n x1, local copies, waits for them, and re-layouts, forward_loop(): masked = jnp.where(inside[None, :], one_loop, jnp.zeros((), one_loop.dtype))  4.15 us
    select_n x1, other arithmetic, forward_loop(): masked = jnp.where(inside[None, :], one_loop, jnp.zeros((), one_loop.dtype))  3.66 us
    dot_general x1, matrix products, inverse_loop(): lax.dot_general(combined.reshape(field_count * block_count, 2 * wave_coun...  3.28 us
    ppermute x15, waiting for transfers between devices, inverse_piece(): lax.ppermute(sent, 'band', [(i, (i + step) % size) for i in range(size)])  2.89 us
    all_to_all x1, waiting for transfers between devices, forward_piece(): lax.all_to_all(loop_piece, 'band', split_axis=1, concat_axis=1, tiled=True)  2.28 us
  transfers between devices with their start and end apart: 16, of which 3 were waited for; matrix products, arithmetic and copies ran while one was open for 4% of the time, Pallas kernels for 0%

profile of v1, /device:TPU:0, one launch (start us, length us, event | category | flops | bytes accessed | tf_op | source)
XLA Modules:
  0.0 84.2 jit_solution(14174149198128723278)
XLA Ops:
  0.0 1.3 %dynamic_slice.108 = s32[1]{0:T(128)} dynamic-slice(s32[16]{0:T(128)} %param.18, s32[]{:T(128)S(6)} %select_n.409), dynamic_slice_sizes={1} | dynamic-slice | bytes 12 | tf_op jit(solution)/shard_map/dynamic_slice | solution.py:124
  3.2 1.3 %dynamic-slice.18 = s32[1]{0:T(128)} dynamic-slice(s32[16]{0:T(128)} %param.17, s32[]{:T(128)} %bitcast), dynamic_slice_sizes={1} | dynamic-slice | bytes 12 | tf_op jit(solution)/shard_map/jit(_take)/gather | solution.py:125
  5.7 3.7 %broadcast_select_fusion = bf16[1,274,5248]{2,1,0:T(8,128)(2,1)} fusion(bf16[1,274,5248]{2,1,0:T(8,128)(2,1)} %param.11, pred[5248]{0:T(1024)(128)(4,1)S(1)} %iota_compare_fusion), kind=kLoop, calls=%fused_computation.6 | loop fusion | flops 1437952 | bytes 5757056 | tf_op jit(solution)/shard_map/while/body/eval_jaxpr/jit(_where)/select_n | solution.py:41
  9.4 4.2 %select_n.416 = bf16[274,41,128]{2,1,0:T(8,128)(2,1)S(1)} reshape(bf16[1,274,5248]{2,1,0:T(8,128)(2,1)} %broadcast_select_fusion) | data formatting | bytes 5751808 | tf_op jit(solution)/shard_map/while/body/eval_jaxpr/jit(_where)/select_n | solution.py:41
  15.5 1.6 %fusion = f32[274,41,2,16]{0,3,2,1:T(8,128)S(1)} fusion(bf16[2,16,128,1]{2,1,0,3:T(8,128)(2,1)S(1)} %bitcast.168, bf16[274,41,128,1]{2,1,0,3:T(8,128)(2,1)S(1)} %bitcast.161), kind=kOutput, calls=%fused_computation.4 | convolution fusion | flops 92028928 | bytes 4322048 | tf_op jit(solution)/shard_map/while/body/eval_jaxpr/dot_general | solution.py:42
  19.8 7.4 %all-to-all-start = ((bf16[16,2,274]{2,1,0:T(2,128)(2,1)}), bf16[16,2,274]{2,1,0:T(2,128)(2,1)S(1)}, u32[]{:S(2)}, u32[]{:S(2)}) async-start(bf16[16,2,274]{2,1,0:T(2,128)(2,1)} %reshape.600), calls=%async_computation | async-start | bytes 49152 | tf_op jit(solution)/shard_map/while/body/eval_jaxpr/all_to_all | solution.py:136
  27.3 1.3 %sort.17 = (s32[16]{0:T(128)}, s32[16]{0:T(128)S(1)}) sort(s32[16]{0:T(128)S(1)} %copy-done.10, s32[16]{0:T(128)S(1)} %iota.42), dimensions={0}, to_apply=%region_2.3 | sort | flops 64 | bytes 256 | tf_op jit(solution)/shard_map/jit(argsort)/sort | solution.py:142
  31.5 2.3 %all-to-all-done = bf16[16,2,274]{2,1,0:T(2,128)(2,1)S(1)} async-done(((bf16[16,2,274]{2,1,0:T(2,128)(2,1)}), bf16[16,2,274]{2,1,0:T(2,128)(2,1)S(1)}, u32[]{:S(2)}, u32[]{:S(2)}) %all-to-all-start) | async-done | bytes 17568 | tf_op jit(solution)/shard_map/while/body/eval_jaxpr/all_to_all | solution.py:136
  35.8 1.4 %copy.34 = f32[2,640,548]{1,0,2:T(2,128)S(1)} copy(f32[2,640,548]{1,2,0:T(8,128)S(1)} %select_bitcast_fusion) | data formatting | bytes 5611520 | tf_op jit(solution)/shard_map/jit(_where)/select_n | solution.py:86
  38.3 1.4 %fusion.8 = f32[2,640,2,137]{1,3,2,0:T(8,128)S(1)} fusion(f32[1,2,640,2,1,137]{2,1,5,4,3,0:T(2,128)S(1)} %get-tuple-element.53, f32[137,137]{1,0:T(8,128)S(1)} %copy-done.1), kind=kOutput, calls=%fused_computation.17 | convolution fusion | flops 576583680 | bytes 2880836 | tf_op jit(solution)/shard_map/...l,kl->...k/dot_general | solution.py:92
  39.7 1.6 %fusion.3 = f32[2,640,2,137]{1,3,2,0:T(8,128)S(1)} fusion(f32[1,2,640,2,1,137]{2,1,5,4,3,0:T(2,128)S(1)} %get-tuple-element.54, f32[2,640,2,137]{1,3,2,0:T(8,128)S(1)} %fusion.8, f32[2,640]{1,0:T(2,128)S(1)} %fusion.57, f32[137,137]{1,0:T(8,128)S(1)} %copy-done), kind=kOutput, calls=%fused_computation.12 | convolution fusion | flops 577285120 | bytes 4288836 | tf_op jit(solution)/shard_map/...l,lk->...k/dot_general | solution.py:95
  41.3 1.6 %fusion.5 = f32[2,640,2,137]{1,3,2,0:T(8,128)S(1)} fusion(f32[2,640,2,137]{1,3,2,0:T(8,128)S(1)} %fusion.3, f32[2,640,137]{1,2,0:T(8,128)S(1)} %multiply_add_fusion, f32[137,137]{1,0:T(8,128)S(1)} %copy-done), kind=kOutput, calls=%fused_computation.14 | convolution fusion | flops 576934400 | bytes 3582276 | tf_op jit(solution)/shard_map/...k,lk->...l/dot_general | solution.py:97
  43.0 1.5 %fusion.11 = bf16[1,2,640,2,1,137]{2,5,3,1,4,0:T(8,128)(2,1)S(1)} fusion(f32[2,640,2,137]{1,3,2,0:T(8,128)S(1)} %fusion.5, f32[1,2,640,2,1,137]{2,1,5,4,3,0:T(2,128)S(1)} %get-tuple-element.53, f32[137,137]{1,0:T(8,128)S(1)} %copy-done.1), kind=kOutput, calls=%fused_computation.20 | convolution fusion | flops 577635840 | bytes 3582276 | tf_op jit(solution)/shard_map/...l,kl->...k/dot_general | solution.py:98
  48.1 1.5 %collective-permute-start.2 = (bf16[1,1,1,548]{3,2,1,0:T(2,128)(2,1)S(1)}, bf16[1,1,1,548]{3,2,1,0:T(2,128)(2,1)S(1)}, u32[]{:S(2)}, u32[]{:S(2)}) collective-permute-start(bf16[1,1,1,548]{3,2,1,0:T(2,128)(2,1)S(1)} %get-tuple-element.75), channel_id=1, source_target_pairs={{0,3},{1,4},{2,5},{3,6},{4,7},{5,8},{6,9},{7,10},{8,11},{9,12},{10... | collective-permute-start | bytes 3296 | tf_op jit(solution)/shard_map/while/body/eval_jaxpr/ppermute | solution.py:170
  49.6 1.5 %collective-permute-start.3 = (bf16[1,1,1,548]{3,2,1,0:T(2,128)(2,1)S(1)}, bf16[1,1,1,548]{3,2,1,0:T(2,128)(2,1)S(1)}, u32[]{:S(2)}, u32[]{:S(2)}) collective-permute-start(bf16[1,1,1,548]{3,2,1,0:T(2,128)(2,1)S(1)} %get-tuple-element.74), channel_id=1, source_target_pairs={{0,4},{1,5},{2,6},{3,7},{4,8},{5,9},{6,10},{7,11},{8,12},{9,13},{1... | collective-permute-start | bytes 3296 | tf_op jit(solution)/shard_map/while/body/eval_jaxpr/ppermute | solution.py:170
  51.2 2.0 %collective-permute-done = bf16[1,1,1,548]{3,2,1,0:T(2,128)(2,1)S(1)} collective-permute-done((bf16[1,1,1,548]{3,2,1,0:T(2,128)(2,1)S(1)}, bf16[1,1,1,548]{3,2,1,0:T(2,128)(2,1)S(1)}, u32[]{:S(2)}, u32[]{:S(2)}) %collective-permute-start) | collective-permute-done | bytes 1128 | tf_op jit(solution)/shard_map/while/body/eval_jaxpr/ppermute | solution.py:170
  54.5 2.4 %collective-permute-start.6 = (bf16[1,1,1,548]{3,2,1,0:T(2,128)(2,1)S(1)}, bf16[1,1,1,548]{3,2,1,0:T(2,128)(2,1)S(1)}, u32[]{:S(2)}, u32[]{:S(2)}) collective-permute-start(bf16[1,1,1,548]{3,2,1,0:T(2,128)(2,1)S(1)} %get-tuple-element.71), channel_id=1, source_target_pairs={{0,7},{1,8},{2,9},{3,10},{4,11},{5,12},{6,13},{7,14},{8,15},{9,0},... | collective-permute-start | bytes 3296 | tf_op jit(solution)/shard_map/while/body/eval_jaxpr/ppermute | solution.py:170
  56.8 1.3 %collective-permute-start.7 = (bf16[1,1,1,548]{3,2,1,0:T(2,128)(2,1)S(1)}, bf16[1,1,1,548]{3,2,1,0:T(2,128)(2,1)S(1)}, u32[]{:S(2)}, u32[]{:S(2)}) collective-permute-start(bf16[1,1,1,548]{3,2,1,0:T(2,128)(2,1)S(1)} %get-tuple-element.70), channel_id=1, source_target_pairs={{0,8},{1,9},{2,10},{3,11},{4,12},{5,13},{6,14},{7,15},{8,0},{9,1},... | collective-permute-start | bytes 3296 | tf_op jit(solution)/shard_map/while/body/eval_jaxpr/ppermute | solution.py:170
  58.1 2.3 %collective-permute-start.9 = (bf16[1,1,1,548]{3,2,1,0:T(2,128)(2,1)S(1)}, bf16[1,1,1,548]{3,2,1,0:T(2,128)(2,1)S(1)}, u32[]{:S(2)}, u32[]{:S(2)}) collective-permute-start(bf16[1,1,1,548]{3,2,1,0:T(2,128)(2,1)S(1)} %get-tuple-element.68), channel_id=1, source_target_pairs={{0,10},{1,11},{2,12},{3,13},{4,14},{5,15},{6,0},{7,1},{8,2},{9,3},... | collective-permute-start | bytes 3296 | tf_op jit(solution)/shard_map/while/body/eval_jaxpr/ppermute | solution.py:170
  60.7 3.4 %collective-permute-start.10 = (bf16[1,1,1,548]{3,2,1,0:T(2,128)(2,1)S(1)}, bf16[1,1,1,548]{3,2,1,0:T(2,128)(2,1)S(1)}, u32[]{:S(2)}, u32[]{:S(2)}) collective-permute-start(bf16[1,1,1,548]{3,2,1,0:T(2,128)(2,1)S(1)} %get-tuple-element.67), channel_id=1, source_target_pairs={{0,11},{1,12},{2,13},{3,14},{4,15},{5,0},{6,1},{7,2},{8,3},{9,4},{... | collective-permute-start | bytes 3296 | tf_op jit(solution)/shard_map/while/body/eval_jaxpr/ppermute | solution.py:170
  66.7 1.9 %collective-permute-start.14 = (bf16[1,1,1,548]{3,2,1,0:T(2,128)(2,1)S(1)}, bf16[1,1,1,548]{3,2,1,0:T(2,128)(2,1)S(1)}, u32[]{:S(2)}, u32[]{:S(2)}) collective-permute-start(bf16[1,1,1,548]{3,2,1,0:T(2,128)(2,1)S(1)} %get-tuple-element.63), channel_id=1, source_target_pairs={{0,15},{1,0},{2,1},{3,2},{4,3},{5,4},{6,5},{7,6},{8,7},{9,8},{10,9... | collective-permute-start | bytes 3296 | tf_op jit(solution)/shard_map/while/body/eval_jaxpr/ppermute | solution.py:170
  73.7 3.3 %fusion.17 = bf16[11234,128]{1,0:T(8,128)(2,1)} fusion(bf16[11234,16]{0,1:T(8,128)(2,1)S(1)} %neg.14, bf16[11234,16]{0,1:T(8,128)(2,1)S(1)} %sub.119, bf16[128,16]{0,1:T(8,128)(2,1)S(1)} %get-tuple-element.81, bf16[128,16]{0,1:T(8,128)(2,1)S(1)} %get-tuple-element.80), kind=kOutput, calls=%fused_computation.32 | convolution fusion | flops 93483264 | bytes 3603072 | tf_op jit(solution)/shard_map/while/body/eval_jaxpr/dot_general | solution.py:68
  76.9 5.2 %reshape.525 = bf16[1,274,5248]{2,1,0:T(8,128)(2,1)S(1)} reshape(bf16[11234,128]{1,0:T(8,128)(2,1)} %fusion.17) | data formatting | bytes 5751808 | tf_op jit(solution)/shard_map/while/body/eval_jaxpr/reshape | solution.py:74
  82.1 2.1 %select_convert_fusion = bf16[1,274,5248]{2,1,0:T(8,128)(2,1)} fusion(bf16[1,274,5248]{2,1,0:T(8,128)(2,1)S(1)} %reshape.525, pred[5248]{0:T(1024)(128)(4,1)S(1)} %iota_compare_fusion), kind=kLoop, calls=%fused_computation.3 | loop fusion | flops 1437952 | bytes 5757056 | tf_op jit(solution)/shard_map/while/body/eval_jaxpr/convert_element_type | solution.py:76
  (116 shorter events, 22.5 us)
Async XLA Ops:
  0.0 39.7 %copy-start = (f32[137,137]{1,0:T(8,128)S(1)}, f32[137,137]{1,0:T(8,128)}, u32[]{:S(2)}) copy-start(f32[137,137]{1,0:T(8,128)} %param.14) | copy-start | bytes 225232
  17.1 10.2 %copy-start.10 = (s32[16]{0:T(128)S(1)}, s32[16]{0:T(128)}, u32[]{:S(2)}) copy-start(s32[16]{0:T(128)} %param.18) | copy-start | bytes 196
  17.1 11.6 %copy-start.6 = (s32[16]{0:T(128)S(1)}, s32[16]{0:T(128)}, u32[]{:S(2)}) copy-start(s32[16]{0:T(128)} %param.19) | copy-start | bytes 196
  17.1 13.7 %copy-start.11 = (s32[16]{0:T(128)S(1)}, s32[16]{0:T(128)}, u32[]{:S(2)}) copy-start(s32[16]{0:T(128)} %param.17) | copy-start | bytes 196
  17.1 13.7 %copy-start.7 = (f32[137]{0:T(256)S(1)}, f32[137]{0:T(256)}, u32[]{:S(2)}) copy-start(f32[137]{0:T(256)} %param.16) | copy-start | bytes 1648
  17.5 17.6 %copy-start.8 = (f32[8]{0:T(128)S(1)}, f32[8]{0:T(128)}, u32[]{:S(2)}) copy-start(f32[8]{0:T(128)} %param.13) | copy-start | bytes 100
  17.5 17.7 %copy-start.4 = (bf16[1,2,640,8]{2,3,1,0:T(8,128)(2,1)S(1)}, bf16[1,2,640,8]{2,3,1,0:T(8,128)(2,1)}, u32[]{:S(2)}) copy-start(bf16[1,2,640,8]{2,3,1,0:T(8,128)(2,1)} %param.12) | copy-start | bytes 61444
  19.8 14.0 %all-to-all-start = ((bf16[16,2,274]{2,1,0:T(2,128)(2,1)}), bf16[16,2,274]{2,1,0:T(2,128)(2,1)S(1)}, u32[]{:S(2)}, u32[]{:S(2)}) async-start(bf16[16,2,274]{2,1,0:T(2,128)(2,1)} %reshape.600), calls=%async_computation | async-start | bytes 49152 | tf_op jit(solution)/shard_map/while/body/eval_jaxpr/all_to_all | solution.py:136
  45.8 24.2 %copy-start.3 = (f32[41,16]{1,0:T(8,128)S(1)}, f32[41,16]{1,0:T(8,128)}, u32[]{:S(2)}) copy-start(f32[41,16]{1,0:T(8,128)} %copy-done.2) | copy-start | bytes 7876
  47.3 6.0 %collective-permute-start = (bf16[1,1,1,548]{3,2,1,0:T(2,128)(2,1)S(1)}, bf16[1,1,1,548]{3,2,1,0:T(2,128)(2,1)S(1)}, u32[]{:S(2)}, u32[]{:S(2)}) collective-permute-start(bf16[1,1,1,548]{3,2,1,0:T(2,128)(2,1)S(1)} %get-tuple-element.77), channel_id=1, source_target_pairs={{0,1},{1,2},{2,3},{3,4},{4,5},{5,6},{6,7},{7,8},{8,9},{9,10},{10,1... | collective-permute-start | bytes 3296 | tf_op jit(solution)/shard_map/while/body/eval_jaxpr/ppermute | solution.py:170
  47.6 6.9 %collective-permute-start.1 = (bf16[1,1,1,548]{3,2,1,0:T(2,128)(2,1)S(1)}, bf16[1,1,1,548]{3,2,1,0:T(2,128)(2,1)S(1)}, u32[]{:S(2)}, u32[]{:S(2)}) collective-permute-start(bf16[1,1,1,548]{3,2,1,0:T(2,128)(2,1)S(1)} %get-tuple-element.76), channel_id=1, source_target_pairs={{0,2},{1,3},{2,4},{3,5},{4,6},{5,7},{6,8},{7,9},{8,10},{9,11},{10,... | collective-permute-start | bytes 3296 | tf_op jit(solution)/shard_map/while/body/eval_jaxpr/ppermute | solution.py:170
  48.1 8.8 %collective-permute-start.2 = (bf16[1,1,1,548]{3,2,1,0:T(2,128)(2,1)S(1)}, bf16[1,1,1,548]{3,2,1,0:T(2,128)(2,1)S(1)}, u32[]{:S(2)}, u32[]{:S(2)}) collective-permute-start(bf16[1,1,1,548]{3,2,1,0:T(2,128)(2,1)S(1)} %get-tuple-element.75), channel_id=1, source_target_pairs={{0,3},{1,4},{2,5},{3,6},{4,7},{5,8},{6,9},{7,10},{8,11},{9,12},{10... | collective-permute-start | bytes 3296 | tf_op jit(solution)/shard_map/while/body/eval_jaxpr/ppermute | solution.py:170
  49.6 8.5 %collective-permute-start.3 = (bf16[1,1,1,548]{3,2,1,0:T(2,128)(2,1)S(1)}, bf16[1,1,1,548]{3,2,1,0:T(2,128)(2,1)S(1)}, u32[]{:S(2)}, u32[]{:S(2)}) collective-permute-start(bf16[1,1,1,548]{3,2,1,0:T(2,128)(2,1)S(1)} %get-tuple-element.74), channel_id=1, source_target_pairs={{0,4},{1,5},{2,6},{3,7},{4,8},{5,9},{6,10},{7,11},{8,12},{9,13},{1... | collective-permute-start | bytes 3296 | tf_op jit(solution)/shard_map/while/body/eval_jaxpr/ppermute | solution.py:170
  51.1 7.1 %collective-permute-start.4 = (bf16[1,1,1,548]{3,2,1,0:T(2,128)(2,1)S(1)}, bf16[1,1,1,548]{3,2,1,0:T(2,128)(2,1)S(1)}, u32[]{:S(2)}, u32[]{:S(2)}) collective-permute-start(bf16[1,1,1,548]{3,2,1,0:T(2,128)(2,1)S(1)} %get-tuple-element.73), channel_id=1, source_target_pairs={{0,5},{1,6},{2,7},{3,8},{4,9},{5,10},{6,11},{7,12},{8,13},{9,14},{... | collective-permute-start | bytes 3296 | tf_op jit(solution)/shard_map/while/body/eval_jaxpr/ppermute | solution.py:170
  53.3 7.4 %collective-permute-start.5 = (bf16[1,1,1,548]{3,2,1,0:T(2,128)(2,1)S(1)}, bf16[1,1,1,548]{3,2,1,0:T(2,128)(2,1)S(1)}, u32[]{:S(2)}, u32[]{:S(2)}) collective-permute-start(bf16[1,1,1,548]{3,2,1,0:T(2,128)(2,1)S(1)} %get-tuple-element.72), channel_id=1, source_target_pairs={{0,6},{1,7},{2,8},{3,9},{4,10},{5,11},{6,12},{7,13},{8,14},{9,15},... | collective-permute-start | bytes 3296 | tf_op jit(solution)/shard_map/while/body/eval_jaxpr/ppermute | solution.py:170
  54.5 9.6 %collective-permute-start.6 = (bf16[1,1,1,548]{3,2,1,0:T(2,128)(2,1)S(1)}, bf16[1,1,1,548]{3,2,1,0:T(2,128)(2,1)S(1)}, u32[]{:S(2)}, u32[]{:S(2)}) collective-permute-start(bf16[1,1,1,548]{3,2,1,0:T(2,128)(2,1)S(1)} %get-tuple-element.71), channel_id=1, source_target_pairs={{0,7},{1,8},{2,9},{3,10},{4,11},{5,12},{6,13},{7,14},{8,15},{9,0},... | collective-permute-start | bytes 3296 | tf_op jit(solution)/shard_map/while/body/eval_jaxpr/ppermute | solution.py:170
  56.8 8.0 %collective-permute-start.7 = (bf16[1,1,1,548]{3,2,1,0:T(2,128)(2,1)S(1)}, bf16[1,1,1,548]{3,2,1,0:T(2,128)(2,1)S(1)}, u32[]{:S(2)}, u32[]{:S(2)}) collective-permute-start(bf16[1,1,1,548]{3,2,1,0:T(2,128)(2,1)S(1)} %get-tuple-element.70), channel_id=1, source_target_pairs={{0,8},{1,9},{2,10},{3,11},{4,12},{5,13},{6,14},{7,15},{8,0},{9,1},... | collective-permute-start | bytes 3296 | tf_op jit(solution)/shard_map/while/body/eval_jaxpr/ppermute | solution.py:170
  58.1 7.4 %collective-permute-start.8 = (bf16[1,1,1,548]{3,2,1,0:T(2,128)(2,1)S(1)}, bf16[1,1,1,548]{3,2,1,0:T(2,128)(2,1)S(1)}, u32[]{:S(2)}, u32[]{:S(2)}) collective-permute-start(bf16[1,1,1,548]{3,2,1,0:T(2,128)(2,1)S(1)} %get-tuple-element.69), channel_id=1, source_target_pairs={{0,9},{1,10},{2,11},{3,12},{4,13},{5,14},{6,15},{7,0},{8,1},{9,2},... | collective-permute-start | bytes 3296 | tf_op jit(solution)/shard_map/while/body/eval_jaxpr/ppermute | solution.py:170
  58.1 8.6 %collective-permute-start.9 = (bf16[1,1,1,548]{3,2,1,0:T(2,128)(2,1)S(1)}, bf16[1,1,1,548]{3,2,1,0:T(2,128)(2,1)S(1)}, u32[]{:S(2)}, u32[]{:S(2)}) collective-permute-start(bf16[1,1,1,548]{3,2,1,0:T(2,128)(2,1)S(1)} %get-tuple-element.68), channel_id=1, source_target_pairs={{0,10},{1,11},{2,12},{3,13},{4,14},{5,15},{6,0},{7,1},{8,2},{9,3},... | collective-permute-start | bytes 3296 | tf_op jit(solution)/shard_map/while/body/eval_jaxpr/ppermute | solution.py:170
  60.7 8.2 %collective-permute-start.10 = (bf16[1,1,1,548]{3,2,1,0:T(2,128)(2,1)S(1)}, bf16[1,1,1,548]{3,2,1,0:T(2,128)(2,1)S(1)}, u32[]{:S(2)}, u32[]{:S(2)}) collective-permute-start(bf16[1,1,1,548]{3,2,1,0:T(2,128)(2,1)S(1)} %get-tuple-element.67), channel_id=1, source_target_pairs={{0,11},{1,12},{2,13},{3,14},{4,15},{5,0},{6,1},{7,2},{8,3},{9,4},{... | collective-permute-start | bytes 3296 | tf_op jit(solution)/shard_map/while/body/eval_jaxpr/ppermute | solution.py:170
  64.1 4.9 %collective-permute-start.11 = (bf16[1,1,1,548]{3,2,1,0:T(2,128)(2,1)S(1)}, bf16[1,1,1,548]{3,2,1,0:T(2,128)(2,1)S(1)}, u32[]{:S(2)}, u32[]{:S(2)}) collective-permute-start(bf16[1,1,1,548]{3,2,1,0:T(2,128)(2,1)S(1)} %get-tuple-element.66), channel_id=1, source_target_pairs={{0,12},{1,13},{2,14},{3,15},{4,0},{5,1},{6,2},{7,3},{8,4},{9,5},{1... | collective-permute-start | bytes 3296 | tf_op jit(solution)/shard_map/while/body/eval_jaxpr/ppermute | solution.py:170
  64.8 4.2 %collective-permute-start.12 = (bf16[1,1,1,548]{3,2,1,0:T(2,128)(2,1)S(1)}, bf16[1,1,1,548]{3,2,1,0:T(2,128)(2,1)S(1)}, u32[]{:S(2)}, u32[]{:S(2)}) collective-permute-start(bf16[1,1,1,548]{3,2,1,0:T(2,128)(2,1)S(1)} %get-tuple-element.65), channel_id=1, source_target_pairs={{0,13},{1,14},{2,15},{3,0},{4,1},{5,2},{6,3},{7,4},{8,5},{9,6},{10... | collective-permute-start | bytes 3296 | tf_op jit(solution)/shard_map/while/body/eval_jaxpr/ppermute | solution.py:170
  65.5 3.6 %collective-permute-start.13 = (bf16[1,1,1,548]{3,2,1,0:T(2,128)(2,1)S(1)}, bf16[1,1,1,548]{3,2,1,0:T(2,128)(2,1)S(1)}, u32[]{:S(2)}, u32[]{:S(2)}) collective-permute-start(bf16[1,1,1,548]{3,2,1,0:T(2,128)(2,1)S(1)} %get-tuple-element.64), channel_id=1, source_target_pairs={{0,14},{1,15},{2,0},{3,1},{4,2},{5,3},{6,4},{7,5},{8,6},{9,7},{10,... | collective-permute-start | bytes 3296 | tf_op jit(solution)/shard_map/while/body/eval_jaxpr/ppermute | solution.py:170
  66.7 3.2 %collective-permute-start.14 = (bf16[1,1,1,548]{3,2,1,0:T(2,128)(2,1)S(1)}, bf16[1,1,1,548]{3,2,1,0:T(2,128)(2,1)S(1)}, u32[]{:S(2)}, u32[]{:S(2)}) collective-permute-start(bf16[1,1,1,548]{3,2,1,0:T(2,128)(2,1)S(1)} %get-tuple-element.63), channel_id=1, source_target_pairs={{0,15},{1,0},{2,1},{3,2},{4,3},{5,4},{6,5},{7,6},{8,7},{9,8},{10,9... | collective-permute-start | bytes 3296 | tf_op jit(solution)/shard_map/while/body/eval_jaxpr/ppermute | solution.py:170
  (4 other events, 7.5 us)
